TPU v7x, 32 devices: a whole 2x2x4 slice. The times are simulated.
32 devices in a mesh: section: 2 (over x), expert: 4 (over y, core), dp: 4 (over z).
Axes of the slice: x: 2, y: 2, z: 4, core: 2. Of those that a mesh axis runs over, the one named last changes fastest.
Arguments:
- arrivals: bfloat16 [2, 1024, 2048], P('section', ('expert', 'dp')), may hold values from -6 to 6
- fresh: bfloat16 [1, 1024, 2048], P(None, ('expert', 'dp')), may hold values from -6 to 6
- routes: int32 [2, 2, 1024, 6], P('section', None, ('expert', 'dp')), may hold values from 0 to 63, as said below
- gates: bfloat16 [2, 2, 1024, 6], P('section', None, ('expert', 'dp')), may hold values from 0.099609375 to 1
- cotangent: bfloat16 [2, 2, 1024, 2048], P('section', None, ('expert', 'dp')), may hold values from -0.3125 to 0.3125
- norm_gain: float32 [2, 2048], P('section'), may hold values from 0.5 to 1.5
- w_gate: bfloat16 [2, 1408, 2048], P('section', 'expert', 'dp'), may hold values from -0.125 to 0.125
- w_up: bfloat16 [2, 1408, 2048], P('section', 'expert', 'dp'), may hold values from -0.125 to 0.125
- w_down: bfloat16 [2, 1408, 2048], P('section', 'expert', 'dp'), may hold values from -0.15625 to 0.15625
Outputs:
- layer_out: bfloat16 [2, 2, 1024, 2048], P('section', None, ('expert', 'dp'))
- grad_down: float32 [2, 1408, 2048], P('section', 'expert', 'dp')
Inputs may be any that keep to these rules, and one draw needn't show every extreme that they name: `routes`: each token's 6 entries are different expert numbers.
All inputs are finite; a program needn't handle non-finite values.
Results may differ from a plain program's by a relative error of at most 0.0085.
Values may be sent and summed in bfloat16 or wider, within the bound.
A program may use at most 64 MiB of HBM per device.

v0:
```python
import jax
import jax.numpy as jnp
from jax import lax
from jax.sharding import PartitionSpec as P

SPLIT = 4
CAP = 12


def shifted_2(shard, axis, by):
    count = lax.axis_size(axis)
    pairs = [(i, i + by) for i in range(count) if 0 <= i + by < count]
    return lax.ppermute(shard, axis, pairs)


def local(arrivals, fresh, routes, gates, cotangent, norm_gain, w_gate, w_up, w_down):
    n_expert = lax.axis_size("expert")
    flight = n_expert // SPLIT
    section_index = lax.axis_index("section")
    tok_rows = arrivals.shape[1]
    model_width = arrivals.shape[2]
    step_count = routes.shape[1]
    gains = norm_gain[0]
    gate_local, up_local, down_local = (
        lax.all_gather(w_gate[0], "dp", axis=1, tiled=True),
        lax.all_gather(w_up[0], "dp", axis=1, tiled=True),
        lax.all_gather(w_down[0], "dp", axis=1, tiled=True),
    )
    hid_rows = gate_local.shape[0]
    slot_ids = jnp.arange(CAP, dtype=jnp.int32)
    expert_ids = jnp.arange(flight, dtype=jnp.int32)
    highest = lax.Precision.HIGHEST
    row_dims = (((0,), (0,)), ((), ()))

    def selection(step_index):
        routing = routes[0, step_index]
        weights = gates[0, step_index].astype(jnp.float32)
        matches = routing[:, :, None] == expert_ids[None, None, :]
        naming = jnp.any(matches, axis=1).astype(jnp.int32)
        shares = jnp.sum(jnp.where(matches, weights[:, :, None], 0.0), axis=1)
        places = jnp.cumsum(naming, axis=0) - naming
        chosen = (naming.T[:, None, :] == 1) & (places.T[:, None, :] == slot_ids[None, :, None])
        select = chosen.reshape(flight * CAP, tok_rows).astype(jnp.bfloat16)
        slot_gate = jnp.sum(jnp.where(chosen, shares.T[:, None, :], 0.0), axis=2).reshape(
            flight * CAP
        )
        counts = jnp.minimum(jnp.sum(naming, axis=0), CAP)
        return (select, slot_gate, counts)

    def fan_out(block_in):
        spread = jnp.broadcast_to(block_in[:, None], (flight, SPLIT) + block_in.shape[1:])
        return spread.reshape((n_expert,) + block_in.shape[1:])

    def pack_rows(select, values):
        rows = jnp.dot(select, values, preferred_element_type=jnp.float32).astype(jnp.bfloat16)
        return fan_out(rows.reshape(flight, CAP, model_width))

    picks = [selection(turn_num) for turn_num in range(step_count)]
    incoming = arrivals[0]
    grad_total = jnp.zeros((hid_rows, model_width), jnp.float32)
    outputs = []
    for turn_num in range(step_count):
        if turn_num > 0:
            shifted = shifted_2(outputs[-1], "section", 1)
            incoming = jnp.where(section_index == 0, fresh[turn_num - 1], shifted)
        floats = incoming.astype(jnp.float32)
        scale = lax.rsqrt(jnp.mean(floats * floats, axis=1, keepdims=True) + 0.5)
        normed = (floats * scale * gains[None, :]).astype(jnp.bfloat16)
        select, slot_gate, counts = picks[turn_num]
        send_tok = pack_rows(select, normed)
        send_cot = pack_rows(select, cotangent[0, turn_num])
        send_gate = fan_out(slot_gate.reshape(flight, CAP).astype(jnp.bfloat16))
        send_count = fan_out(counts)
        rows_tok, rows_cot, rows_gate, rows_count = (
            lax.all_to_all(send_tok, "expert", split_axis=0, concat_axis=0, tiled=True),
            lax.all_to_all(send_cot, "expert", split_axis=0, concat_axis=0, tiled=True),
            lax.all_to_all(send_gate, "expert", split_axis=0, concat_axis=0, tiled=True),
            lax.all_to_all(send_count, "expert", split_axis=0, concat_axis=0, tiled=True),
        )
        total_rows = n_expert * CAP
        flat_tok = rows_tok.reshape(total_rows, model_width)
        flat_cot = rows_cot.reshape(total_rows, model_width)
        flat_gate = rows_gate.reshape(total_rows)
        dims = (((1,), (1,)), ((), ()))
        gate_act = lax.dot_general(flat_tok, gate_local, dims, preferred_element_type=jnp.float32)
        up_act = lax.dot_general(flat_tok, up_local, dims, preferred_element_type=jnp.float32)
        hidden = (jax.nn.silu(gate_act) * up_act).astype(jnp.bfloat16)
        partial_value = jnp.dot(hidden, down_local, preferred_element_type=jnp.float32).astype(
            jnp.bfloat16
        )
        weighted = (hidden.astype(jnp.float32) * flat_gate.astype(jnp.float32)[:, None]).astype(
            jnp.bfloat16
        )
        expert_partial_value = partial_value
        grad_add = lax.dot_general(weighted, flat_cot, row_dims, preferred_element_type=jnp.float32)
        partial_value, grad_add = (
            expert_partial_value.reshape(n_expert, CAP, model_width),
            grad_add,
        )
        returned = lax.all_to_all(partial_value, "expert", split_axis=0, concat_axis=0, tiled=True)
        expert_out = jnp.sum(
            returned.reshape(flight, SPLIT, CAP, model_width).astype(jnp.float32), axis=1
        ).reshape(flight * CAP, model_width)
        mixing = select.astype(jnp.float32).T * slot_gate[None, :]
        mixture = jnp.dot(mixing, expert_out, precision=highest)
        result = (floats + mixture).astype(jnp.bfloat16)
        outputs.append(result)
        grad_total = grad_total + grad_add
    grad_part = lax.psum_scatter(grad_total, "dp", scatter_dimension=1, tiled=True)
    return (jnp.stack(outputs)[None], grad_part[None])


def solution(mesh):
    placed = (
        P("section", ("expert", "dp"), None),
        P(None, ("expert", "dp"), None),
        P("section", None, ("expert", "dp"), None),
        P("section", None, ("expert", "dp"), None),
        P("section", None, ("expert", "dp"), None),
        P("section", None),
        P("section", "expert", "dp"),
        P("section", "expert", "dp"),
        P("section", "expert", "dp"),
    )
    return jax.shard_map(
        local,
        mesh=mesh,
        in_specs=placed,
        out_specs=(P("section", None, ("expert", "dp"), None), P("section", "expert", "dp")),
        check_vma=False,
    )
```

profile of v0, /device:TPU:0, one launch (start us, length us, event | category | flops | bytes accessed | tf_op | source)
XLA Modules:
  0.0 242.2 jit_solution(11923948752257591277)
XLA Ops:
  7.3 0.7 all-gather.7.cloned.1.call-update
  7.9 0.0 all-gather.9.cloned.1.call-start
  8.0 0.7 all-gather.9.cloned.1.call-update
  8.7 0.0 all-gather.11.cloned.1.call-start
  8.7 0.7 all-gather.11.cloned.1.call-update
  9.4 0.8 compare_reduce_fusion
  10.2 0.1 copy.17
  10.3 0.1 reduce-window.14
  10.4 0.1 reduce.14
  10.5 1.1 fusion.26
  11.7 0.2 convolution_convert_fusion.5
  11.9 0.7 reshape.550
  12.7 4.3 %all-to-all-start = ((bf16[4,12,2048]{2,1,0:T(8,128)(2,1)}), bf16[4,12,2048]{2,1,0:T(8,128)(2,1)S(1)}, u32[]{:S(2)}, u32[]{:S(2)}) async-start(bf16[4,12,2048]{2,1,0:T(8,128)(2,1)} %reshape.550), calls=%async_computation | async-start | bytes 524288 | tf_op jit(solution)/shard_map/all_to_all | solution.py:75
  16.9 0.1 copy.18
  17.0 0.1 reduce-window.15
  17.1 0.1 reduce.15
  17.3 0.2 fusion.69
  17.5 0.2 fusion.68
  17.7 5.3 %all-to-all-done = bf16[4,12,2048]{2,1,0:T(8,128)(2,1)S(1)} async-done(((bf16[4,12,2048]{2,1,0:T(8,128)(2,1)}), bf16[4,12,2048]{2,1,0:T(8,128)(2,1)S(1)}, u32[]{:S(2)}, u32[]{:S(2)}) %all-to-all-start) | async-done | bytes 196640 | tf_op jit(solution)/shard_map/all_to_all | solution.py:75
  23.0 24.1 %all-gather.7.cloned.1.call-done = bf16[1,352,2048]{2,1,0:T(8,128)(2,1)} async-done(((bf16[1,352,512]{2,1,0:T(8,128)(2,1)}), bf16[1,352,2048]{2,1,0:T(8,128)(2,1)}) %all-gather.7.cloned.1.call-update) | async-done | bytes 1441808 | tf_op jit(solution)/shard_map/all_gather | solution.py:25
  47.0 1.9 fusion.11
  49.0 33.5 %all-gather.9.cloned.1.call-done = bf16[1,352,2048]{2,1,0:T(8,128)(2,1)} async-done(((bf16[1,352,512]{2,1,0:T(8,128)(2,1)}), bf16[1,352,2048]{2,1,0:T(8,128)(2,1)}) %all-gather.9.cloned.1.call-update) | async-done | bytes 1441808 | tf_op jit(solution)/shard_map/all_gather | solution.py:26
  82.5 1.9 fusion.22
  84.4 33.4 %all-gather.11.cloned.1.call-done = bf16[1,352,2048]{2,1,0:T(8,128)(2,1)} async-done(((bf16[1,352,512]{2,1,0:T(8,128)(2,1)}), bf16[1,352,2048]{2,1,0:T(8,128)(2,1)}) %all-gather.11.cloned.1.call-update) | async-done | bytes 1441808 | tf_op jit(solution)/shard_map/all_gather | solution.py:27
  117.8 1.7 convolution_convert_fusion.1
  119.6 0.8 reshape.552
  120.3 3.4 %all-to-all-start.1 = ((bf16[4,12,2048]{2,1,0:T(8,128)(2,1)}), bf16[4,12,2048]{2,1,0:T(8,128)(2,1)S(1)}, u32[]{:S(2)}, u32[]{:S(2)}) async-start(bf16[4,12,2048]{2,1,0:T(8,128)(2,1)} %reshape.552), calls=%async_computation.1 | async-start | bytes 524288 | tf_op jit(solution)/shard_map/all_to_all | solution.py:100
  123.7 0.1 convolution_convert_fusion.3
  123.9 5.8 %all-to-all-done.1 = bf16[4,12,2048]{2,1,0:T(8,128)(2,1)S(1)} async-done(((bf16[4,12,2048]{2,1,0:T(8,128)(2,1)}), bf16[4,12,2048]{2,1,0:T(8,128)(2,1)S(1)}, u32[]{:S(2)}, u32[]{:S(2)}) %all-to-all-start.1) | async-done | bytes 196640 | tf_op jit(solution)/shard_map/all_to_all | solution.py:100
  129.7 0.6 reshape.557
  130.3 3.2 %all-to-all-start.4 = ((bf16[4,1,12]{2,1,0:T(2,128)(2,1)}), bf16[4,1,12]{2,1,0:T(2,128)(2,1)S(1)}, u32[]{:S(2)}, u32[]{:S(2)}) async-start(bf16[4,1,12]{2,1,0:T(2,128)(2,1)} %reshape.557), calls=%async_computation.4 | async-start | bytes 4096 | tf_op jit(solution)/shard_map/all_to_all | solution.py:77
  133.6 0.6 fusion
  134.2 3.0 %all-to-all-done.4 = bf16[4,1,12]{2,1,0:T(2,128)(2,1)S(1)} async-done(((bf16[4,1,12]{2,1,0:T(2,128)(2,1)}), bf16[4,1,12]{2,1,0:T(2,128)(2,1)S(1)}, u32[]{:S(2)}, u32[]{:S(2)}) %all-to-all-start.4) | async-done | bytes 128 | tf_op jit(solution)/shard_map/all_to_all | solution.py:77
  137.2 0.6 reshape.560
  137.8 3.2 %all-to-all-start.6 = ((bf16[4,1,12]{2,1,0:T(2,128)(2,1)}), bf16[4,1,12]{2,1,0:T(2,128)(2,1)S(1)}, u32[]{:S(2)}, u32[]{:S(2)}) async-start(bf16[4,1,12]{2,1,0:T(2,128)(2,1)} %reshape.560), calls=%async_computation.6 | async-start | bytes 4096 | tf_op jit(solution)/shard_map/all_to_all | solution.py:77
  141.0 3.5 %collective-permute-start = (bf16[64,2048]{1,0:T(8,128)(2,1)S(1)}, bf16[64,2048]{1,0:T(8,128)(2,1)S(1)}, u32[]{:S(2)}, u32[]{:S(2)}) collective-permute-start(bf16[64,2048]{1,0:T(8,128)(2,1)S(1)} %fusion), channel_id=1, source_target_pairs={{0,16},{1,17},{2,18},{3,19},{4,20},{5,21},{6,22},{7,23},{8,24},{9,... | collective-permute-start | bytes 786440 | tf_op jit(solution)/shard_map/ppermute | solution.py:13
  144.5 0.1 all-to-all-done.6
  144.7 0.7 reshape.558
  145.4 3.4 %all-to-all-start.5 = ((bf16[4,12,2048]{2,1,0:T(8,128)(2,1)}), bf16[4,12,2048]{2,1,0:T(8,128)(2,1)S(1)}, u32[]{:S(2)}, u32[]{:S(2)}) async-start(bf16[4,12,2048]{2,1,0:T(8,128)(2,1)} %reshape.558), calls=%async_computation.5 | async-start | bytes 524288 | tf_op jit(solution)/shard_map/all_to_all | solution.py:76
  148.8 0.1 convolution_convert_fusion.2
  149.0 5.8 %all-to-all-done.5 = bf16[4,12,2048]{2,1,0:T(8,128)(2,1)S(1)} async-done(((bf16[4,12,2048]{2,1,0:T(8,128)(2,1)}), bf16[4,12,2048]{2,1,0:T(8,128)(2,1)S(1)}, u32[]{:S(2)}, u32[]{:S(2)}) %all-to-all-start.5) | async-done | bytes 196640 | tf_op jit(solution)/shard_map/all_to_all | solution.py:76
  154.8 0.7 reshape.561
  155.5 3.4 %all-to-all-start.7 = ((bf16[4,12,2048]{2,1,0:T(8,128)(2,1)}), bf16[4,12,2048]{2,1,0:T(8,128)(2,1)S(1)}, u32[]{:S(2)}, u32[]{:S(2)}) async-start(bf16[4,12,2048]{2,1,0:T(8,128)(2,1)} %reshape.561), calls=%async_computation.7 | async-start | bytes 524288 | tf_op jit(solution)/shard_map/all_to_all | solution.py:76
  158.9 0.1 reshape.566
  159.0 0.7 reshape.567
  159.8 5.1 %all-to-all-done.7 = bf16[4,12,2048]{2,1,0:T(8,128)(2,1)S(1)} async-done(((bf16[4,12,2048]{2,1,0:T(8,128)(2,1)}), bf16[4,12,2048]{2,1,0:T(8,128)(2,1)S(1)}, u32[]{:S(2)}, u32[]{:S(2)}) %all-to-all-start.7) | async-done | bytes 196640 | tf_op jit(solution)/shard_map/all_to_all | solution.py:76
  165.0 0.2 fusion.29
  165.2 0.7 copy-done.3
  165.9 0.2 convolution_convert_fusion.4
  166.1 0.7 reshape.554
  166.8 3.4 %all-to-all-start.2 = ((bf16[4,12,2048]{2,1,0:T(8,128)(2,1)}), bf16[4,12,2048]{2,1,0:T(8,128)(2,1)S(1)}, u32[]{:S(2)}, u32[]{:S(2)}) async-start(bf16[4,12,2048]{2,1,0:T(8,128)(2,1)} %reshape.554), calls=%async_computation.2 | async-start | bytes 524288 | tf_op jit(solution)/shard_map/all_to_all | solution.py:75
  170.3 0.0 reduce-scatter.2.cloned.1.call-start
  170.3 1.4 fusion.43
  171.7 4.5 %all-to-all-done.2 = bf16[4,12,2048]{2,1,0:T(8,128)(2,1)S(1)} async-done(((bf16[4,12,2048]{2,1,0:T(8,128)(2,1)}), bf16[4,12,2048]{2,1,0:T(8,128)(2,1)S(1)}, u32[]{:S(2)}, u32[]{:S(2)}) %all-to-all-start.2) | async-done | bytes 196640 | tf_op jit(solution)/shard_map/all_to_all | solution.py:75
  176.3 2.0 fusion.9
  178.3 0.6 fusion.19
  178.9 2.2 convolution_add_fusion
  181.2 1.3 copy-done
  182.5 0.4 convolution_convert_fusion
  182.9 0.1 reshape.556
  182.9 8.4 %all_to_all.42 = bf16[4,12,2048]{2,1,0:T(8,128)(2,1)S(1)} all-to-all(bf16[4,12,2048]{2,1,0:T(8,128)(2,1)S(1)} %reshape.556), channel_id=1, replica_groups=mesh['section'=2,'expert'=4,'dp'=4] {'expert'}, dimensions={0} | all-to-all | bytes 393216 | tf_op jit(solution)/shard_map/all_to_all | solution.py:100
  191.4 0.6 fusion.2
  192.0 0.8 maximum_bitcast_fusion
  192.9 42.8 %reduce-scatter.2.cloned.1.call-done = f32[352,512]{1,0:T(8,128)} async-done(((f32[352,2048]{1,0:T(8,128)}), f32[352,512]{1,0:T(8,128)}) %reduce-scatter.2.cloned.1.call-update) | async-done | bytes 720912 | tf_op jit(solution)/shard_map/reduce_scatter | solution.py:109
  (46 shorter events, 0.5 us)
Async XLA Ops:
  7.2 10.1 %copy-start.10 = (s32[1,2,64,6]{2,1,3,0:T(2,128)S(1)}, s32[1,2,64,6]{2,1,3,0:T(2,128)}, u32[]{:S(2)}) copy-start(s32[1,2,64,6]{2,1,3,0:T(2,128)} %param.11) | copy-start | bytes 9220
  7.2 4.5 %copy-start.2 = (bf16[1,64,2048]{2,1,0:T(8,128)(2,1)S(1)}, bf16[1,64,2048]{2,1,0:T(8,128)(2,1)}, u32[]{:S(2)}) copy-start(bf16[1,64,2048]{2,1,0:T(8,128)(2,1)} %param.9) | copy-start | bytes 786436
  7.2 4.5 %copy-start.13 = (f32[1,2048]{1,0:T(1,128)S(1)}, f32[1,2048]{1,0:T(1,128)}, u32[]{:S(2)}) copy-start(f32[1,2048]{1,0:T(1,128)} %param.14) | copy-start | bytes 24580
  7.2 10.1 %copy-start.11 = (bf16[1,2,64,6]{2,1,3,0:T(2,128)(2,1)S(1)}, bf16[1,2,64,6]{2,1,3,0:T(2,128)(2,1)}, u32[]{:S(2)}) copy-start(bf16[1,2,64,6]{2,1,3,0:T(2,128)(2,1)} %param.12) | copy-start | bytes 4612
  7.2 39.8 %all-gather.7.cloned.1.call-start = ((), (), s32[]{:S(2)}) async-start(), calls=%async_computation.10 | async-start | bytes 1802240 | tf_op jit(solution)/shard_map/all_gather | solution.py:25
  7.9 74.5 %all-gather.9.cloned.1.call-start = ((), (), s32[]{:S(2)}) async-start(), calls=%async_computation.11 | async-start | bytes 1802240 | tf_op jit(solution)/shard_map/all_gather | solution.py:26
  8.7 109.1 %all-gather.11.cloned.1.call-start = ((), (), s32[]{:S(2)}) async-start(), calls=%async_computation.12 | async-start | bytes 1802240 | tf_op jit(solution)/shard_map/all_gather | solution.py:27
  12.7 10.3 %all-to-all-start = ((bf16[4,12,2048]{2,1,0:T(8,128)(2,1)}), bf16[4,12,2048]{2,1,0:T(8,128)(2,1)S(1)}, u32[]{:S(2)}, u32[]{:S(2)}) async-start(bf16[4,12,2048]{2,1,0:T(8,128)(2,1)} %reshape.550), calls=%async_computation | async-start | bytes 524288 | tf_op jit(solution)/shard_map/all_to_all | solution.py:75
  84.4 35.9 %copy-start.8 = (bf16[48,352]{1,0:T(8,128)(2,1)}, bf16[48,352]{1,0:T(8,128)(2,1)S(1)}, u32[]{:S(2)}) copy-start(bf16[48,352]{1,0:T(8,128)(2,1)S(1)} %fusion.22) | copy-start | bytes 101380
  84.4 39.3 %copy-start.7 = (bf16[1,2,64,2048]{3,2,1,0:T(8,128)(2,1)S(1)}, bf16[1,2,64,2048]{3,2,1,0:T(8,128)(2,1)}, u32[]{:S(2)}) copy-start(bf16[1,2,64,2048]{3,2,1,0:T(8,128)(2,1)} %param.13) | copy-start | bytes 1572868
  120.3 9.4 %all-to-all-start.1 = ((bf16[4,12,2048]{2,1,0:T(8,128)(2,1)}), bf16[4,12,2048]{2,1,0:T(8,128)(2,1)S(1)}, u32[]{:S(2)}, u32[]{:S(2)}) async-start(bf16[4,12,2048]{2,1,0:T(8,128)(2,1)} %reshape.552), calls=%async_computation.1 | async-start | bytes 524288 | tf_op jit(solution)/shard_map/all_to_all | solution.py:100
  130.3 6.9 %all-to-all-start.4 = ((bf16[4,1,12]{2,1,0:T(2,128)(2,1)}), bf16[4,1,12]{2,1,0:T(2,128)(2,1)S(1)}, u32[]{:S(2)}, u32[]{:S(2)}) async-start(bf16[4,1,12]{2,1,0:T(2,128)(2,1)} %reshape.557), calls=%async_computation.4 | async-start | bytes 4096 | tf_op jit(solution)/shard_map/all_to_all | solution.py:77
  134.2 30.7 %copy-start.5 = (bf16[64,2048]{1,0:T(8,128)(2,1)}, bf16[64,2048]{1,0:T(8,128)(2,1)S(1)}, u32[]{:S(2)}) copy-start(bf16[64,2048]{1,0:T(8,128)(2,1)S(1)} %fusion) | copy-start | bytes 786436
  137.8 6.9 %all-to-all-start.6 = ((bf16[4,1,12]{2,1,0:T(2,128)(2,1)}), bf16[4,1,12]{2,1,0:T(2,128)(2,1)S(1)}, u32[]{:S(2)}, u32[]{:S(2)}) async-start(bf16[4,1,12]{2,1,0:T(2,128)(2,1)} %reshape.560), calls=%async_computation.6 | async-start | bytes 4096 | tf_op jit(solution)/shard_map/all_to_all | solution.py:77
  141.0 24.0 %copy-start.9 = (bf16[1,64,2048]{2,1,0:T(8,128)(2,1)S(1)}, bf16[1,64,2048]{2,1,0:T(8,128)(2,1)}, u32[]{:S(2)}) copy-start(bf16[1,64,2048]{2,1,0:T(8,128)(2,1)} %param.10) | copy-start | bytes 786436
  141.0 23.9 %collective-permute-start = (bf16[64,2048]{1,0:T(8,128)(2,1)S(1)}, bf16[64,2048]{1,0:T(8,128)(2,1)S(1)}, u32[]{:S(2)}, u32[]{:S(2)}) collective-permute-start(bf16[64,2048]{1,0:T(8,128)(2,1)S(1)} %fusion), channel_id=1, source_target_pairs={{0,16},{1,17},{2,18},{3,19},{4,20},{5,21},{6,22},{7,23},{8,24},{9,... | collective-permute-start | bytes 786440 | tf_op jit(solution)/shard_map/ppermute | solution.py:13
  145.4 9.4 %all-to-all-start.5 = ((bf16[4,12,2048]{2,1,0:T(8,128)(2,1)}), bf16[4,12,2048]{2,1,0:T(8,128)(2,1)S(1)}, u32[]{:S(2)}, u32[]{:S(2)}) async-start(bf16[4,12,2048]{2,1,0:T(8,128)(2,1)} %reshape.558), calls=%async_computation.5 | async-start | bytes 524288 | tf_op jit(solution)/shard_map/all_to_all | solution.py:76
  155.5 9.4 %all-to-all-start.7 = ((bf16[4,12,2048]{2,1,0:T(8,128)(2,1)}), bf16[4,12,2048]{2,1,0:T(8,128)(2,1)S(1)}, u32[]{:S(2)}, u32[]{:S(2)}) async-start(bf16[4,12,2048]{2,1,0:T(8,128)(2,1)} %reshape.561), calls=%async_computation.7 | async-start | bytes 524288 | tf_op jit(solution)/shard_map/all_to_all | solution.py:76
  165.2 0.7 copy-start.3
  166.8 9.4 %all-to-all-start.2 = ((bf16[4,12,2048]{2,1,0:T(8,128)(2,1)}), bf16[4,12,2048]{2,1,0:T(8,128)(2,1)S(1)}, u32[]{:S(2)}, u32[]{:S(2)}) async-start(bf16[4,12,2048]{2,1,0:T(8,128)(2,1)} %reshape.554), calls=%async_computation.2 | async-start | bytes 524288 | tf_op jit(solution)/shard_map/all_to_all | solution.py:75
  170.3 65.5 %reduce-scatter.2.cloned.1.call-start = ((), (), s32[]{:S(2)}) async-start(), calls=%async_computation.9 | async-start | bytes 3604480 | tf_op jit(solution)/shard_map/reduce_scatter | solution.py:109
  176.3 2.1 copy-start.1
  176.3 2.6 %copy-start.12 = (f32[48]{0:T(128)S(1)}, f32[48]{0:T(128)}, u32[]{:S(2)}) copy-start(f32[48]{0:T(128)} %reshape.567) | copy-start | bytes 580
  181.1 1.4 copy-start
  182.5 8.9 %copy-start.4 = (bf16[64,2048]{1,0:T(8,128)(2,1)S(1)}, bf16[64,2048]{1,0:T(8,128)(2,1)}, u32[]{:S(2)}) copy-start(bf16[64,2048]{1,0:T(8,128)(2,1)} %copy-done.3) | copy-start | bytes 786436
  182.5 9.5 %copy-start.6 = (bf16[64,2048]{1,0:T(8,128)(2,1)S(1)}, bf16[64,2048]{1,0:T(8,128)(2,1)}, u32[]{:S(2)}) copy-start(bf16[64,2048]{1,0:T(8,128)(2,1)} %copy-done.5) | copy-start | bytes 786436
Sparse Core Ops, SparseCore 0:
  9.6 37.4 all-gather.6
  48.6 33.8 all-gather.8
  84.0 33.7 all-gather.10
  181.3 54.3 reduce-scatter.1
where the time goes:
time: 243 us; the launch traced here: 242 us
  waiting for transfers between devices  166 us (68%)
  starting transfers between devices  28 us (12%)
  matrix products  14.2 us (6%)
  between operations  14.2 us (6%)
  blocking collectives  8.39 us (3%)
  local copies, waits for them, and re-layouts  8.09 us (3%)
  other arithmetic  3.92 us (2%)
    reduce_scatter x1, waiting for transfers between devices, local(): lax.psum_scatter(grad_total, 'dp', scatter_dimension=1, tiled=True)  42.8 us
    all_gather x1, waiting for transfers between devices, local(): lax.all_gather(w_up[0], 'dp', axis=1, tiled=True)  33.5 us
    all_gather x1, waiting for transfers between devices, local(): lax.all_gather(w_down[0], 'dp', axis=1, tiled=True)  33.4 us
    all_gather x1, waiting for transfers between devices, local(): lax.all_gather(w_gate[0], 'dp', axis=1, tiled=True)  24.1 us
    all_to_all x2, waiting for transfers between devices, local(): lax.all_to_all(send_cot, 'expert', split_axis=0, concat_axis=0, tiled=True)  10.9 us
    all_to_all x2, waiting for transfers between devices, local(): lax.all_to_all(send_tok, 'expert', split_axis=0, concat_axis=0, tiled=True)  9.79 us
    all_to_all x1, blocking collectives, local(): lax.all_to_all(partial_value, 'expert', split_axis=0, concat_axis=0, tile...  8.39 us
    all_to_all x2, starting transfers between devices, local(): lax.all_to_all(send_tok, 'expert', split_axis=0, concat_axis=0, tiled=True)  7.67 us
  transfers between devices with their start and end apart: 12, of which 11 were waited for; matrix products, arithmetic and copies ran while one was open for 6% of the time, Pallas kernels for 0%

commit v1 on v0

--- a/solution.py
+++ b/solution.py
@@ -23,7 +23,7 @@
     gains = norm_gain[0]
     gate_local, up_local, down_local = (
         lax.all_gather(w_gate[0], "dp", axis=1, tiled=True),
-        lax.all_gather(w_up[0], "dp", axis=1, tiled=True),
+        jnp.concatenate(lax.all_gather(w_up[0], "dp"), axis=1),
         lax.all_gather(w_down[0], "dp", axis=1, tiled=True),
     )
     hid_rows = gate_local.shape[0]

time: 243 us -> 243 us (level)
    all_gather x1, waiting for transfers between devices: 24.1 us -> 33.9 us  [local(): lax.all_gather(w_gate[0], 'dp', axis=1, tiled=True)]
    all_gather x1, waiting for transfers between devices: 33.5 us -> 24 us  [local(): lax.all_gather(w_up[0], 'dp')]
  transfers between devices with their start and end apart: 12 -> 12, of which waited for: 11 -> 10; matrix products, arithmetic and copies ran while one was open for 6% -> 7% of each run, Pallas kernels for 0% -> 0%
where the time goes in v1:
time: 243 us; the launch traced here: 242 us
  waiting for transfers between devices  164 us (67%)
  starting transfers between devices  28.7 us (12%)
  between operations  14.2 us (6%)
  matrix products  13 us (5%)
  local copies, waits for them, and re-layouts  10.2 us (4%)
  blocking collectives  8.39 us (3%)
  other arithmetic  3.92 us (2%)
    reduce_scatter x1, waiting for transfers between devices, local(): lax.psum_scatter(grad_total, 'dp', scatter_dimension=1, tiled=True)  43.3 us
    all_gather x1, waiting for transfers between devices, local(): lax.all_gather(w_gate[0], 'dp', axis=1, tiled=True)  33.9 us
    all_gather x1, waiting for transfers between devices, local(): lax.all_gather(w_down[0], 'dp', axis=1, tiled=True)  32.8 us
    all_gather x1, waiting for transfers between devices, local(): lax.all_gather(w_up[0], 'dp')  24 us
    all_to_all x2, waiting for transfers between devices, local(): lax.all_to_all(send_cot, 'expert', split_axis=0, concat_axis=0, tiled=True)  11 us
    all_to_all x1, blocking collectives, local(): lax.all_to_all(partial_value, 'expert', split_axis=0, concat_axis=0, tile...  8.39 us
    all_to_all x2, waiting for transfers between devices, local(): lax.all_to_all(send_tok, 'expert', split_axis=0, concat_axis=0, tiled=True)  8.1 us
    all_to_all x2, starting transfers between devices, local(): lax.all_to_all(send_tok, 'expert', split_axis=0, concat_axis=0, tiled=True)  7.67 us
  transfers between devices with their start and end apart: 12, of which 10 were waited for; matrix products, arithmetic and copies ran while one was open for 7% of the time, Pallas kernels for 0%

profile of v1, /device:TPU:0, one launch (start us, length us, event | category | flops | bytes accessed | tf_op | source)
XLA Modules:
  0.0 242.4 jit_solution(4790391423137975508)
XLA Ops:
  7.3 0.7 all-gather.6.cloned.1.call-update
  7.9 0.0 all-gather.8.cloned.1.call-start
  8.0 0.7 all-gather.8.cloned.1.call-update
  8.7 0.7 all-gather.10.cloned.1.call-update
  9.4 0.8 compare_reduce_fusion
  10.2 0.1 copy.19
  10.3 0.1 reduce-window.14
  10.4 0.1 reduce.14
  10.5 1.1 fusion.12
  11.7 0.2 convolution_convert_fusion.5
  11.9 0.7 reshape.556
  12.7 4.3 %all-to-all-start = ((bf16[4,12,2048]{2,1,0:T(8,128)(2,1)}), bf16[4,12,2048]{2,1,0:T(8,128)(2,1)S(1)}, u32[]{:S(2)}, u32[]{:S(2)}) async-start(bf16[4,12,2048]{2,1,0:T(8,128)(2,1)} %reshape.556), calls=%async_computation | async-start | bytes 524288 | tf_op jit(solution)/shard_map/all_to_all | solution.py:75
  16.9 0.1 copy.21
  17.0 0.1 reduce-window.15
  17.1 0.1 reduce.15
  17.3 0.2 fusion.55
  17.5 0.2 fusion.54
  17.7 5.3 %all-to-all-done = bf16[4,12,2048]{2,1,0:T(8,128)(2,1)S(1)} async-done(((bf16[4,12,2048]{2,1,0:T(8,128)(2,1)}), bf16[4,12,2048]{2,1,0:T(8,128)(2,1)S(1)}, u32[]{:S(2)}, u32[]{:S(2)}) %all-to-all-start) | async-done | bytes 196640 | tf_op jit(solution)/shard_map/all_to_all | solution.py:75
  23.0 24.0 %all-gather.6.cloned.1.call-done = bf16[4,352,512]{2,1,0:T(8,128)(2,1)} async-done(((bf16[1,352,512]{2,1,0:T(8,128)(2,1)}), bf16[4,352,512]{2,1,0:T(8,128)(2,1)}) %all-gather.6.cloned.1.call-update) | async-done | bytes 1441808 | tf_op jit(solution)/shard_map/all_gather | solution.py:26
  47.0 1.5 copy.22
  48.6 33.9 %all-gather.8.cloned.1.call-done = bf16[1,352,2048]{2,1,0:T(8,128)(2,1)} async-done(((bf16[1,352,512]{2,1,0:T(8,128)(2,1)}), bf16[1,352,2048]{2,1,0:T(8,128)(2,1)}) %all-gather.8.cloned.1.call-update) | async-done | bytes 1441808 | tf_op jit(solution)/shard_map/all_gather | solution.py:25
  82.5 1.9 fusion.7
  84.4 0.6 fusion.9
  85.0 32.8 %all-gather.10.cloned.1.call-done = bf16[1,352,2048]{2,1,0:T(8,128)(2,1)} async-done(((bf16[1,352,512]{2,1,0:T(8,128)(2,1)}), bf16[1,352,2048]{2,1,0:T(8,128)(2,1)}) %all-gather.10.cloned.1.call-update) | async-done | bytes 1441808 | tf_op jit(solution)/shard_map/all_gather | solution.py:27
  117.8 1.7 convolution_convert_fusion.1
  119.5 0.8 reshape.560
  120.3 3.4 %all-to-all-start.1 = ((bf16[4,12,2048]{2,1,0:T(8,128)(2,1)}), bf16[4,12,2048]{2,1,0:T(8,128)(2,1)S(1)}, u32[]{:S(2)}, u32[]{:S(2)}) async-start(bf16[4,12,2048]{2,1,0:T(8,128)(2,1)} %reshape.560), calls=%async_computation.1 | async-start | bytes 524288 | tf_op jit(solution)/shard_map/all_to_all | solution.py:100
  123.7 0.1 convolution_convert_fusion.3
  123.9 5.8 %all-to-all-done.1 = bf16[4,12,2048]{2,1,0:T(8,128)(2,1)S(1)} async-done(((bf16[4,12,2048]{2,1,0:T(8,128)(2,1)}), bf16[4,12,2048]{2,1,0:T(8,128)(2,1)S(1)}, u32[]{:S(2)}, u32[]{:S(2)}) %all-to-all-start.1) | async-done | bytes 196640 | tf_op jit(solution)/shard_map/all_to_all | solution.py:100
  129.7 0.6 reshape.565
  130.3 3.2 %all-to-all-start.4 = ((bf16[4,1,12]{2,1,0:T(2,128)(2,1)}), bf16[4,1,12]{2,1,0:T(2,128)(2,1)S(1)}, u32[]{:S(2)}, u32[]{:S(2)}) async-start(bf16[4,1,12]{2,1,0:T(2,128)(2,1)} %reshape.565), calls=%async_computation.4 | async-start | bytes 4096 | tf_op jit(solution)/shard_map/all_to_all | solution.py:77
  133.6 0.6 fusion
  134.2 3.0 %all-to-all-done.4 = bf16[4,1,12]{2,1,0:T(2,128)(2,1)S(1)} async-done(((bf16[4,1,12]{2,1,0:T(2,128)(2,1)}), bf16[4,1,12]{2,1,0:T(2,128)(2,1)S(1)}, u32[]{:S(2)}, u32[]{:S(2)}) %all-to-all-start.4) | async-done | bytes 128 | tf_op jit(solution)/shard_map/all_to_all | solution.py:77
  137.2 0.6 reshape.568
  137.8 3.2 %all-to-all-start.6 = ((bf16[4,1,12]{2,1,0:T(2,128)(2,1)}), bf16[4,1,12]{2,1,0:T(2,128)(2,1)S(1)}, u32[]{:S(2)}, u32[]{:S(2)}) async-start(bf16[4,1,12]{2,1,0:T(2,128)(2,1)} %reshape.568), calls=%async_computation.6 | async-start | bytes 4096 | tf_op jit(solution)/shard_map/all_to_all | solution.py:77
  141.0 4.2 %collective-permute-start = (bf16[64,2048]{1,0:T(8,128)(2,1)S(1)}, bf16[64,2048]{1,0:T(8,128)(2,1)}, u32[]{:S(2)}, u32[]{:S(2)}) collective-permute-start(bf16[64,2048]{1,0:T(8,128)(2,1)S(1)} %fusion), channel_id=1, source_target_pairs={{0,16},{1,17},{2,18},{3,19},{4,20},{5,21},{6,22},{7,23},{8,24},{9,... | collective-permute-start | bytes 786440 | tf_op jit(solution)/shard_map/ppermute | solution.py:13
  145.2 0.7 reshape.566
  145.9 3.4 %all-to-all-start.5 = ((bf16[4,12,2048]{2,1,0:T(8,128)(2,1)}), bf16[4,12,2048]{2,1,0:T(8,128)(2,1)S(1)}, u32[]{:S(2)}, u32[]{:S(2)}) async-start(bf16[4,12,2048]{2,1,0:T(8,128)(2,1)} %reshape.566), calls=%async_computation.5 | async-start | bytes 524288 | tf_op jit(solution)/shard_map/all_to_all | solution.py:76
  149.3 0.1 convolution_convert_fusion.2
  149.5 5.8 %all-to-all-done.5 = bf16[4,12,2048]{2,1,0:T(8,128)(2,1)S(1)} async-done(((bf16[4,12,2048]{2,1,0:T(8,128)(2,1)}), bf16[4,12,2048]{2,1,0:T(8,128)(2,1)S(1)}, u32[]{:S(2)}, u32[]{:S(2)}) %all-to-all-start.5) | async-done | bytes 196640 | tf_op jit(solution)/shard_map/all_to_all | solution.py:76
  155.3 0.7 reshape.569
  156.0 3.4 %all-to-all-start.7 = ((bf16[4,12,2048]{2,1,0:T(8,128)(2,1)}), bf16[4,12,2048]{2,1,0:T(8,128)(2,1)S(1)}, u32[]{:S(2)}, u32[]{:S(2)}) async-start(bf16[4,12,2048]{2,1,0:T(8,128)(2,1)} %reshape.569), calls=%async_computation.7 | async-start | bytes 524288 | tf_op jit(solution)/shard_map/all_to_all | solution.py:76
  159.5 0.1 reshape.574
  159.6 0.6 reshape.575
  160.2 5.2 %all-to-all-done.7 = bf16[4,12,2048]{2,1,0:T(8,128)(2,1)S(1)} async-done(((bf16[4,12,2048]{2,1,0:T(8,128)(2,1)}), bf16[4,12,2048]{2,1,0:T(8,128)(2,1)S(1)}, u32[]{:S(2)}, u32[]{:S(2)}) %all-to-all-start.7) | async-done | bytes 196640 | tf_op jit(solution)/shard_map/all_to_all | solution.py:76
  165.5 0.2 fusion.15
  165.7 0.7 copy-done.4
  166.4 0.2 convolution_convert_fusion.4
  166.7 0.7 reshape.562
  167.4 3.4 %all-to-all-start.2 = ((bf16[4,12,2048]{2,1,0:T(8,128)(2,1)}), bf16[4,12,2048]{2,1,0:T(8,128)(2,1)S(1)}, u32[]{:S(2)}, u32[]{:S(2)}) async-start(bf16[4,12,2048]{2,1,0:T(8,128)(2,1)} %reshape.562), calls=%async_computation.2 | async-start | bytes 524288 | tf_op jit(solution)/shard_map/all_to_all | solution.py:75
  170.8 0.0 reduce-scatter.2.cloned.1.call-start
  170.9 3.1 %fusion.29 = f32[352,2048]{1,0:T(8,128)} fusion(bf16[48,2048]{1,0:T(8,128)(2,1)S(1)} %reshape.567, bf16[48,352]{1,0:T(8,128)(2,1)} %copy-done.9, f32[48]{0:T(128)S(1)} %reshape.574), kind=kOutput, calls=%fused_computation.48 | convolution fusion | flops 69256704 | bytes 3114176 | tf_op jit(solution)/shard_map/dot_general | solution.py:95
  174.0 2.8 %all-to-all-done.2 = bf16[4,12,2048]{2,1,0:T(8,128)(2,1)S(1)} async-done(((bf16[4,12,2048]{2,1,0:T(8,128)(2,1)}), bf16[4,12,2048]{2,1,0:T(8,128)(2,1)S(1)}, u32[]{:S(2)}, u32[]{:S(2)}) %all-to-all-start.2) | async-done | bytes 196640 | tf_op jit(solution)/shard_map/all_to_all | solution.py:75
  176.9 0.6 fusion.5
  177.4 0.6 fusion.10
  178.0 0.7 copy-done
  178.7 2.2 convolution_add_fusion
  180.9 1.3 copy-done.1
  182.2 0.4 convolution_convert_fusion
  182.6 0.1 reshape.564
  182.7 8.4 %all_to_all.42 = bf16[4,12,2048]{2,1,0:T(8,128)(2,1)S(1)} all-to-all(bf16[4,12,2048]{2,1,0:T(8,128)(2,1)S(1)} %reshape.564), channel_id=1, replica_groups=mesh['section'=2,'expert'=4,'dp'=4] {'expert'}, dimensions={0} | all-to-all | bytes 393216 | tf_op jit(solution)/shard_map/all_to_all | solution.py:100
  191.1 0.6 fusion.2
  191.8 0.8 maximum_bitcast_fusion
  192.6 43.3 %reduce-scatter.2.cloned.1.call-done = f32[352,512]{1,0:T(8,128)} async-done(((f32[352,2048]{1,0:T(8,128)}), f32[352,512]{1,0:T(8,128)}) %reduce-scatter.2.cloned.1.call-update) | async-done | bytes 720912 | tf_op jit(solution)/shard_map/reduce_scatter | solution.py:109
  (49 shorter events, 0.6 us)
Async XLA Ops:
  7.2 10.1 %copy-start.11 = (s32[1,2,64,6]{2,1,3,0:T(2,128)S(1)}, s32[1,2,64,6]{2,1,3,0:T(2,128)}, u32[]{:S(2)}) copy-start(s32[1,2,64,6]{2,1,3,0:T(2,128)} %param.11) | copy-start | bytes 9220
  7.2 4.5 %copy-start.3 = (bf16[1,64,2048]{2,1,0:T(8,128)(2,1)S(1)}, bf16[1,64,2048]{2,1,0:T(8,128)(2,1)}, u32[]{:S(2)}) copy-start(bf16[1,64,2048]{2,1,0:T(8,128)(2,1)} %param.9) | copy-start | bytes 786436
  7.2 4.5 %copy-start.14 = (f32[1,2048]{1,0:T(1,128)S(1)}, f32[1,2048]{1,0:T(1,128)}, u32[]{:S(2)}) copy-start(f32[1,2048]{1,0:T(1,128)} %param.14) | copy-start | bytes 24580
  7.2 10.1 %copy-start.12 = (bf16[1,2,64,6]{2,1,3,0:T(2,128)(2,1)S(1)}, bf16[1,2,64,6]{2,1,3,0:T(2,128)(2,1)}, u32[]{:S(2)}) copy-start(bf16[1,2,64,6]{2,1,3,0:T(2,128)(2,1)} %param.12) | copy-start | bytes 4612
  7.2 39.8 %all-gather.6.cloned.1.call-start = ((), (), s32[]{:S(2)}) async-start(), calls=%async_computation.9 | async-start | bytes 1802240 | tf_op jit(solution)/shard_map/all_gather | solution.py:26
  7.9 74.5 %all-gather.8.cloned.1.call-start = ((), (), s32[]{:S(2)}) async-start(), calls=%async_computation.11 | async-start | bytes 1802240 | tf_op jit(solution)/shard_map/all_gather | solution.py:25
  8.7 109.1 %all-gather.10.cloned.1.call-start = ((), (), s32[]{:S(2)}) async-start(), calls=%async_computation.12 | async-start | bytes 1802240 | tf_op jit(solution)/shard_map/all_gather | solution.py:27
  12.7 10.3 %all-to-all-start = ((bf16[4,12,2048]{2,1,0:T(8,128)(2,1)}), bf16[4,12,2048]{2,1,0:T(8,128)(2,1)S(1)}, u32[]{:S(2)}, u32[]{:S(2)}) async-start(bf16[4,12,2048]{2,1,0:T(8,128)(2,1)} %reshape.556), calls=%async_computation | async-start | bytes 524288 | tf_op jit(solution)/shard_map/all_to_all | solution.py:75
  85.0 35.3 %copy-start.9 = (bf16[48,352]{1,0:T(8,128)(2,1)}, bf16[48,352]{1,0:T(8,128)(2,1)S(1)}, u32[]{:S(2)}) copy-start(bf16[48,352]{1,0:T(8,128)(2,1)S(1)} %fusion.9) | copy-start | bytes 101380
  85.0 38.8 %copy-start.8 = (bf16[1,2,64,2048]{3,2,1,0:T(8,128)(2,1)S(1)}, bf16[1,2,64,2048]{3,2,1,0:T(8,128)(2,1)}, u32[]{:S(2)}) copy-start(bf16[1,2,64,2048]{3,2,1,0:T(8,128)(2,1)} %param.13) | copy-start | bytes 1572868
  120.3 9.4 %all-to-all-start.1 = ((bf16[4,12,2048]{2,1,0:T(8,128)(2,1)}), bf16[4,12,2048]{2,1,0:T(8,128)(2,1)S(1)}, u32[]{:S(2)}, u32[]{:S(2)}) async-start(bf16[4,12,2048]{2,1,0:T(8,128)(2,1)} %reshape.560), calls=%async_computation.1 | async-start | bytes 524288 | tf_op jit(solution)/shard_map/all_to_all | solution.py:100
  130.3 6.9 %all-to-all-start.4 = ((bf16[4,1,12]{2,1,0:T(2,128)(2,1)}), bf16[4,1,12]{2,1,0:T(2,128)(2,1)S(1)}, u32[]{:S(2)}, u32[]{:S(2)}) async-start(bf16[4,1,12]{2,1,0:T(2,128)(2,1)} %reshape.565), calls=%async_computation.4 | async-start | bytes 4096 | tf_op jit(solution)/shard_map/all_to_all | solution.py:77
  134.2 31.3 %copy-start.6 = (bf16[64,2048]{1,0:T(8,128)(2,1)}, bf16[64,2048]{1,0:T(8,128)(2,1)S(1)}, u32[]{:S(2)}) copy-start(bf16[64,2048]{1,0:T(8,128)(2,1)S(1)} %fusion) | copy-start | bytes 786436
  137.8 7.4 %all-to-all-start.6 = ((bf16[4,1,12]{2,1,0:T(2,128)(2,1)}), bf16[4,1,12]{2,1,0:T(2,128)(2,1)S(1)}, u32[]{:S(2)}, u32[]{:S(2)}) async-start(bf16[4,1,12]{2,1,0:T(2,128)(2,1)} %reshape.568), calls=%async_computation.6 | async-start | bytes 4096 | tf_op jit(solution)/shard_map/all_to_all | solution.py:77
  141.0 24.5 %copy-start.10 = (bf16[1,64,2048]{2,1,0:T(8,128)(2,1)S(1)}, bf16[1,64,2048]{2,1,0:T(8,128)(2,1)}, u32[]{:S(2)}) copy-start(bf16[1,64,2048]{2,1,0:T(8,128)(2,1)} %param.10) | copy-start | bytes 786436
  141.0 24.5 %collective-permute-start = (bf16[64,2048]{1,0:T(8,128)(2,1)S(1)}, bf16[64,2048]{1,0:T(8,128)(2,1)}, u32[]{:S(2)}, u32[]{:S(2)}) collective-permute-start(bf16[64,2048]{1,0:T(8,128)(2,1)S(1)} %fusion), channel_id=1, source_target_pairs={{0,16},{1,17},{2,18},{3,19},{4,20},{5,21},{6,22},{7,23},{8,24},{9,... | collective-permute-start | bytes 786440 | tf_op jit(solution)/shard_map/ppermute | solution.py:13
  145.9 9.4 %all-to-all-start.5 = ((bf16[4,12,2048]{2,1,0:T(8,128)(2,1)}), bf16[4,12,2048]{2,1,0:T(8,128)(2,1)S(1)}, u32[]{:S(2)}, u32[]{:S(2)}) async-start(bf16[4,12,2048]{2,1,0:T(8,128)(2,1)} %reshape.566), calls=%async_computation.5 | async-start | bytes 524288 | tf_op jit(solution)/shard_map/all_to_all | solution.py:76
  156.0 9.4 %all-to-all-start.7 = ((bf16[4,12,2048]{2,1,0:T(8,128)(2,1)}), bf16[4,12,2048]{2,1,0:T(8,128)(2,1)S(1)}, u32[]{:S(2)}, u32[]{:S(2)}) async-start(bf16[4,12,2048]{2,1,0:T(8,128)(2,1)} %reshape.569), calls=%async_computation.7 | async-start | bytes 524288 | tf_op jit(solution)/shard_map/all_to_all | solution.py:76
  165.7 0.7 copy-start.4
  167.4 9.4 %all-to-all-start.2 = ((bf16[4,12,2048]{2,1,0:T(8,128)(2,1)}), bf16[4,12,2048]{2,1,0:T(8,128)(2,1)S(1)}, u32[]{:S(2)}, u32[]{:S(2)}) async-start(bf16[4,12,2048]{2,1,0:T(8,128)(2,1)} %reshape.562), calls=%async_computation.2 | async-start | bytes 524288 | tf_op jit(solution)/shard_map/all_to_all | solution.py:75
  170.8 6.0 %copy-start.2 = (bf16[1,352,2048]{2,1,0:T(8,128)(2,1)S(1)}, bf16[1,352,2048]{2,1,0:T(8,128)(2,1)}, u32[]{:S(2)}) copy-start(bf16[1,352,2048]{2,1,0:T(8,128)(2,1)} %all-gather.8.cloned.1.call-done) | copy-start | bytes 4325380
  170.8 65.0 %reduce-scatter.2.cloned.1.call-start = ((), (), s32[]{:S(2)}) async-start(), calls=%async_computation.10 | async-start | bytes 3604480 | tf_op jit(solution)/shard_map/reduce_scatter | solution.py:109
  176.8 1.8 copy-start
  176.9 1.8 copy-start.13
  180.9 1.4 copy-start.1
  182.2 8.9 %copy-start.5 = (bf16[64,2048]{1,0:T(8,128)(2,1)S(1)}, bf16[64,2048]{1,0:T(8,128)(2,1)}, u32[]{:S(2)}) copy-start(bf16[64,2048]{1,0:T(8,128)(2,1)} %copy-done.4) | copy-start | bytes 786436
  182.2 9.5 %copy-start.7 = (bf16[64,2048]{1,0:T(8,128)(2,1)S(1)}, bf16[64,2048]{1,0:T(8,128)(2,1)}, u32[]{:S(2)}) copy-start(bf16[64,2048]{1,0:T(8,128)(2,1)} %copy-done.6) | copy-start | bytes 786436
Sparse Core Ops, SparseCore 0:
  9.6 37.4 all-gather.5
  48.6 33.8 all-gather.7
  84.0 33.7 all-gather.9
  181.0 54.8 reduce-scatter.1
